TPU v7x, 32 devices: a whole 2x2x4 slice. The times are simulated.
32 devices in a mesh: dp: 8 (over z, y), mp: 4 (over x, core).
Axes of the slice: x: 2, y: 2, z: 4, core: 2. Of those that a mesh axis runs over, the one named last changes fastest.
Arguments:
- gradient: bfloat16 [8, 64, 14336], P('dp', None, 'mp'), may hold values from -6 to 6
- momentum: float32 [8, 64, 14336], P('dp', None, 'mp'), may hold values from -6 to 6
- weights: float32 [64, 14336], P(None, 'mp'), may hold values from -6 to 6
- positions: int32 [8, 1, 224, 32], P('dp', None, 'mp'), may hold values from 0 to 4095, as said below
Outputs:
- new_momentum: float32 [8, 64, 14336], P('dp', None, 'mp')
- new_weights: float32 [64, 14336], P(None, 'mp')
Inputs may be any that keep to these rules, and one draw needn't show every extreme that they name: Within one span of one replica the 32 positions are all different.
All inputs are finite; a program needn't handle non-finite values.
Results may differ from a plain program's by a relative error of at most 0.0003.
Values sent between devices are 32-bit elements; how exact they have to be, the bound alone decides.
No kernel may reach another device: no remote copies, remote signals or barrier semaphores. Data moves between devices by JAX's collectives and lax.ppermute only.
A program may use at most 64 MiB of HBM per device.

v0:
```python
import math
import jax
import jax.numpy as jnp
from jax import lax
from jax.sharding import PartitionSpec as P

FF = 14336


def dct_table():
    column = jnp.arange(64, dtype=jnp.float32)
    freq = column[:, None]
    factor = jnp.where(freq == 0, jnp.sqrt(jnp.float32(1.0 / 64)), jnp.sqrt(jnp.float32(2.0 / 64)))
    return factor * jnp.cos(jnp.pi * (2.0 * column[None, :] + 1.0) * freq / 128.0)


def paired_table(table):
    ident = jnp.eye(2, dtype=jnp.float32)
    return (ident[:, None, :, None] * table[None, :, None, :]).reshape(128, 128)


def forward_dct(field, table, paired):
    bands, height, width = field.shape
    along = jnp.einsum("kr,brf->bkf", table, field, precision=lax.Precision.HIGHEST)
    grouped = along.reshape(bands, height, width // 128, 128)
    result = jnp.einsum("bkgs,ls->bkgl", grouped, paired, precision=lax.Precision.HIGHEST)
    return result.reshape(bands, height, width)


def inverse_dct(coefs, table, paired):
    bands, height, width = coefs.shape
    grouped = coefs.reshape(bands, height, width // 128, 128)
    across = jnp.einsum("bkgl,ls->bkgs", grouped, paired, precision=lax.Precision.HIGHEST)
    across = across.reshape(bands, height, width)
    return jnp.einsum("kr,bkf->brf", table, across, precision=lax.Precision.HIGHEST)


def to_spans(field):
    bands, height, width = field.shape
    split = field.reshape(bands, 64, width // 64, 64)
    return jnp.transpose(split, (0, 2, 1, 3))


def from_spans(spans):
    bands, count, height, width = spans.shape
    return jnp.transpose(spans, (0, 2, 1, 3)).reshape(bands, 64, count * 64)


def decode_group(values, places):
    freqs = jnp.arange(64, dtype=jnp.int32)
    row_hot = (places[..., None] // 64 == freqs).astype(jnp.float32) * values[..., None]
    col_hot = (places[..., None] % 64 == freqs).astype(jnp.float32)
    return jnp.einsum("nbcjk,nbcjl->bckl", row_hot, col_hot, precision=lax.Precision.HIGHEST)


def decode_lists(values, places):
    count = values.shape[0]
    group = math.gcd(count, 8)
    steps = count // group
    if steps == 1:
        return decode_group(values, places)

    def add_group(index, total):
        part_values = lax.dynamic_slice_in_dim(values, index * group, group, 0)
        part_places = lax.dynamic_slice_in_dim(places, index * group, group, 0)
        return total + decode_group(part_values, part_places)

    start = jnp.zeros((values.shape[1], values.shape[2], 64, 64), jnp.float32)
    return lax.fori_loop(0, steps, add_group, start)


def local(gradient, momentum, weights, positions):
    table = dct_table()
    paired = paired_table(table)
    summed = 0.9 * momentum[0] + gradient[0].astype(jnp.float32)
    bands = summed.shape[0] // 64
    count = summed.shape[1] // 64
    coefs = forward_dct(summed.reshape(bands, 64, summed.shape[1]), table, paired)
    flattened = to_spans(coefs).reshape(bands, count, 4096)
    own_places = positions[0]
    picked = jnp.take_along_axis(flattened, own_places, axis=2)
    own = decode_group(picked[None], own_places[None])
    back = inverse_dct(from_spans(own), table, paired)
    new_momentum = (summed - back.reshape(summed.shape))[None]
    aggregate = decode_lists(
        lax.all_gather(picked[None], "dp", axis=0, tiled=True),
        lax.all_gather(own_places[None].astype(jnp.float32), "dp", axis=0, tiled=True).astype(
            jnp.int32
        ),
    )
    update = inverse_dct(from_spans(aggregate), table, paired).reshape(weights.shape)
    total_sq = lax.psum(jnp.sum(update * update), "mp")
    meansq = total_sq / (weights.shape[0] * FF)
    new_weights = weights - update / jnp.sqrt(meansq + 1.0)
    return (new_momentum, new_weights)


def solution(mesh):
    placed = (P("dp", None, "mp"), P("dp", None, "mp"), P(None, "mp"), P("dp", None, "mp", None))
    return jax.shard_map(
        local,
        mesh=mesh,
        in_specs=placed,
        out_specs=(P("dp", None, "mp"), P(None, "mp")),
        check_vma=False,
    )
```

profile of v0, /device:TPU:0, one launch (start us, length us, event | category | flops | bytes accessed | tf_op | source)
XLA Modules:
  0.0 132.9 jit_solution(11840959320905657482)
XLA Ops:
  0.7 0.8 fusion.34
  1.7 0.7 convert_element_type.28
  2.4 0.8 copy.30
  3.6 32.3 %all_gather.6 = f32[8,1,56,32]{2,3,1,0:T(8,128)S(1)} all-gather(f32[1,1,56,32]{2,3,1,0:T(8,128)S(1)} %convert_element_type.28), channel_id=1, replica_groups=mesh['dp'=8,'mp'=4] {'dp'}, dimensions={0}, use_global_device_ids=true | all-gather | bytes 64512 | tf_op jit(solution)/shard_map/all_gather | solution.py:87
  36.0 0.8 copy.38
  36.9 0.8 copy.44
  37.7 1.2 convolution_bitcast_fusion.1
  39.1 1.5 %fusion.18 = f32[64,28,128]{2,0,1:T(8,128)S(1)} fusion(f32[128,128,1]{1,0,2:T(8,128)S(1)} %reshape.454, f32[64,28,128]{2,1,0:T(8,128)S(1)} %reshape.436), kind=kOutput, calls=%fused_computation.25 | convolution fusion | flops 352321536 | bytes 1900544 | tf_op jit(solution)/shard_map/bkgs,ls->bkgl/dot_general | solution.py:26
  40.5 0.5 copy.32
  41.1 0.3 reshape_reshape.2
  41.4 1.6 %copy.33 = f32[1,56,64,64]{3,2,1,0:T(8,128)} copy(f32[1,56,64,64]{3,1,2,0:T(8,128)S(1)} %bitcast.113) | data formatting | bytes 1835008 | tf_op jit(solution)/shard_map/transpose | solution.py:41
  43.0 2.1 %reshape.442 = f32[56,4096]{1,0:T(8,128)S(1)} reshape(f32[1,56,64,64]{3,2,1,0:T(8,128)} %copy.33) | data formatting | bytes 1835008 | tf_op jit(solution)/shard_map/reshape | solution.py:79
  45.1 14.0 %gather_fusion = f32[1792]{0:T(1024)S(1)} fusion(f32[56,4096]{1,0:T(8,128)S(1)} %reshape.442, s32[1792]{0:T(1024)S(1)} %reshape.444), kind=kCustom, calls=%fused_computation | custom fusion | bytes 28672 | tf_op jit(solution)/shard_map/jit(take_along_axis)/gather | solution.py:81
  59.3 30.5 %all_gather.7 = f32[8,1,56,32]{2,3,1,0:T(8,128)S(1)} all-gather(f32[1,1,56,32]{2,3,1,0:T(8,128)S(1)} %copy.42), channel_id=1, replica_groups=mesh['dp'=8,'mp'=4] {'dp'}, dimensions={0}, use_global_device_ids=true | all-gather | bytes 64512 | tf_op jit(solution)/shard_map/all_gather | solution.py:86
  90.0 22.1 %fusion.7 = f32[1,64,56,64]{3,1,2,0:T(8,128)S(1)} fusion(s32[8,56,32]{2,0,1:T(8,128)S(1)} %copy-done.5, f32[8,56,32]{2,0,1:T(8,128)S(1)} %copy.43, s32[8,56,32]{2,0,1:T(8,128)S(1)} %copy-done.4), kind=kOutput, calls=%fused_computation.13 | convolution fusion | flops 707395584 | bytes 1089536 | tf_op jit(solution)/shard_map/nbcjk,nbcjl->bckl/dot_general | solution.py:53
  112.1 1.1 copy.45
  113.5 1.5 %convolution_bitcast_fusion.3 = f32[28,8,8,128]{3,2,1,0:T(8,128)S(1)} fusion(f32[128,128,1]{1,0,2:T(8,128)S(1)} %reshape.454, f32[64,28,128]{2,1,0:T(8,128)S(1)} %reshape.440), kind=kOutput, calls=%fused_computation.14 | convolution fusion | flops 352321536 | bytes 1900544 | tf_op jit(solution)/shard_map/bkgl,ls->bkgs/dot_general | solution.py:33
  114.9 1.8 %multiply_reduce_fusion = (f32[]{:T(128)}, f32[3584,64]{0,1:T(8,128)S(1)}) fusion(f32[64]{0:T(128)S(1)} %get-tuple-element.9, f32[64]{0:T(128)S(1)} %get-tuple-element.8, f32[28,8,8,128]{3,2,1,0:T(8,128)S(1)} %convolution_bitcast_fusion.3), kind=kOutput, calls=%fused_computation.27 | convolution fusion | flops 176631808 | bytes 1835524 | tf_op jit(solution)/shard_map/kr,bkf->brf/dot_general | solution.py:35
  116.7 6.4 %psum.7 = f32[]{:T(128)} all-reduce(f32[]{:T(128)} %get-tuple-element.6), channel_id=1, replica_groups=mesh['dp'=8,'mp'=4] {'mp'}, use_global_device_ids=true, to_apply=%region_1.2 | all-reduce | flops 1 | bytes 8 | tf_op jit(solution)/shard_map/psum | solution.py:92
  123.9 1.0 bitcast_subtract_fusion
  124.9 3.1 %convolution_bitcast_fusion.2 = f32[1,64,56,64]{3,1,2,0:T(8,128)S(1)} fusion(s32[56,32]{1,0:T(8,128)S(1)} %get-tuple-element.5, f32[56,32]{1,0:T(8,128)S(1)} %and_select_fusion.1, s32[56,32]{1,0:T(8,128)S(1)} %get-tuple-element.4), kind=kOutput, calls=%fused_computation.12 | convolution fusion | flops 88424448 | bytes 939008 | tf_op jit(solution)/shard_map/nbcjk,nbcjl->bckl/dot_general | solution.py:53
  127.9 1.1 copy.35
  129.3 1.5 %convolution_bitcast_fusion.4 = f32[28,8,8,128]{3,2,1,0:T(8,128)S(1)} fusion(f32[128,128,1]{1,0,2:T(8,128)S(1)} %reshape.454, f32[64,28,128]{2,1,0:T(8,128)S(1)} %reshape.438), kind=kOutput, calls=%fused_computation.15 | convolution fusion | flops 352321536 | bytes 1900544 | tf_op jit(solution)/shard_map/bkgl,ls->bkgs/dot_general | solution.py:33
  130.8 2.0 %fusion.2 = f32[1,64,3584]{2,1,0:T(8,128)} fusion(f32[28,8,8,128]{3,2,1,0:T(8,128)S(1)} %convolution_bitcast_fusion.4, bf16[1,64,3584]{2,1,0:T(8,128)(2,1)S(1)} %copy-done.2, f32[1,64,3584]{2,1,0:T(8,128)S(1)} %copy-done.1, f32[64]{0:T(128)S(1)} %get-tuple-element.9, f32[64]{0:T(128)S(1)} %get-tuple-element.8), kind=kOutput, calls=%fused_computation.7 | convolution fusion | flops 177090560 | bytes 3211776 | tf_op jit(solution)/shard_map/kr,bkf->brf/dot_general | solution.py:35
  (30 shorter events, 1.9 us)
Async XLA Ops:
  0.6 37.0 %copy-start = (f32[1,64,3584]{2,1,0:T(8,128)S(1)}, f32[1,64,3584]{2,1,0:T(8,128)}, u32[]{:S(2)}) copy-start(f32[1,64,3584]{2,1,0:T(8,128)} %param.5) | copy-start | bytes 2752516
  0.6 37.0 %copy-start.2 = (bf16[1,64,3584]{2,1,0:T(8,128)(2,1)S(1)}, bf16[1,64,3584]{2,1,0:T(8,128)(2,1)}, u32[]{:S(2)}) copy-start(bf16[1,64,3584]{2,1,0:T(8,128)(2,1)} %param.4) | copy-start | bytes 1376260
  45.1 44.9 %copy-start.4 = (s32[8,56,32]{2,0,1:T(8,128)S(1)}, s32[8,56,32]{2,0,1:T(8,128)}, u32[]{:S(2)}) copy-start(s32[8,56,32]{2,0,1:T(8,128)} %copy.38) | copy-start | bytes 172036
  45.1 44.9 %copy-start.5 = (s32[8,56,32]{2,0,1:T(8,128)S(1)}, s32[8,56,32]{2,0,1:T(8,128)}, u32[]{:S(2)}) copy-start(s32[8,56,32]{2,0,1:T(8,128)} %copy.44) | copy-start | bytes 172036
  114.9 8.9 %copy-start.3 = (f32[64,3584]{1,0:T(8,128)S(1)}, f32[64,3584]{1,0:T(8,128)}, u32[]{:S(2)}) copy-start(f32[64,3584]{1,0:T(8,128)} %param.6) | copy-start | bytes 2752516
  129.3 1.5 %copy-start.1 = (f32[1,64,3584]{2,1,0:T(8,128)S(1)}, f32[1,64,3584]{2,1,0:T(8,128)}, u32[]{:S(2)}) copy-start(f32[1,64,3584]{2,1,0:T(8,128)} %param.5) | copy-start | bytes 2752516
where the time goes:
time: 133 us
  blocking collectives  69.3 us (52%)
  matrix products  34.5 us (26%)
  local copies, waits for them, and re-layouts  24.5 us (18%)
  other arithmetic  3.01 us (2%)
  between operations  1.57 us (1%)
    all_gather x1, blocking collectives, local(): lax.all_gather(own_places[None].astype(jnp.float32), 'dp', axis=0, tiled=...  32.3 us
    all_gather x1, blocking collectives, local(): lax.all_gather(picked[None], 'dp', axis=0, tiled=True)  30.5 us
    dot_general x2, matrix products, decode_group(): jnp.einsum('nbcjk,nbcjl->bckl', row_hot, col_hot, precision=lax.Precision...  25.1 us
    gather x5, local copies, waits for them, and re-layouts, local(): picked = jnp.take_along_axis(flattened, own_places, axis=2)  14.3 us
    psum x1, blocking collectives, local(): total_sq = lax.psum(jnp.sum(update * update), 'mp')  6.45 us
    dot_general x2, matrix products, inverse_dct(): jnp.einsum('kr,bkf->brf', table, across, precision=lax.Precision.HIGHEST)  3.8 us
    dot_general x2, matrix products, inverse_dct(): jnp.einsum('bkgl,ls->bkgs', grouped, paired, precision=lax.Precision.HIGH...  2.93 us

commit v1 on v0

--- a/solution.py
+++ b/solution.py
@@ -5,6 +5,13 @@
 from jax.sharding import PartitionSpec as P
 
 FF = 14336
+
+
+def swapped_in(block, name, along):
+    size = lax.axis_size(name)
+    parts = jnp.stack([block for _ in range(size)])
+    parts = lax.all_to_all(parts, name, split_axis=0, concat_axis=0)
+    return jnp.concatenate(parts, axis=along)
 
 
 def dct_table():
@@ -83,7 +90,7 @@
     back = inverse_dct(from_spans(own), table, paired)
     new_momentum = (summed - back.reshape(summed.shape))[None]
     aggregate = decode_lists(
-        lax.all_gather(picked[None], "dp", axis=0, tiled=True),
+        swapped_in(picked[None], "dp", 0),
         lax.all_gather(own_places[None].astype(jnp.float32), "dp", axis=0, tiled=True).astype(
             jnp.int32
         ),

time: 133 us -> 111 us (0.83)
  blocking collectives: 69.3 us -> 37.5 us
  starting transfers between devices: 0 us -> 7.31 us
    all_gather x1 -> x0, blocking collectives: 30.5 us -> none  [local(): lax.all_gather(picked[None], 'dp', axis=0, tiled=True)]
    all_to_all x0 -> x1, starting transfers between devices: none -> 7.31 us  [swapped_in(): parts = lax.all_to_all(parts, name, split_axis=0, concat_axis=0)]
    all_to_all x0 -> x1, other arithmetic: none -> 1.6 us  [swapped_in(): parts = lax.all_to_all(parts, name, split_axis=0, concat_axis=0)]
  transfers between devices with their start and end apart: 0 -> 1, of which waited for: 0 -> 0; matrix products, arithmetic and copies ran while one was open for 0% -> 8% of each run, Pallas kernels for 0% -> 0%
where the time goes in v1:
time: 111 us
  blocking collectives  37.5 us (34%)
  matrix products  35.8 us (32%)
  local copies, waits for them, and re-layouts  24.6 us (22%)
  starting transfers between devices  7.31 us (7%)
  other arithmetic  3.79 us (3%)
  between operations  1.61 us (1%)
    all_gather x1, blocking collectives, local(): lax.all_gather(own_places[None].astype(jnp.float32), 'dp', axis=0, tiled=...  31.2 us
    dot_general x2, matrix products, decode_group(): jnp.einsum('nbcjk,nbcjl->bckl', row_hot, col_hot, precision=lax.Precision...  25.2 us
    gather x5, local copies, waits for them, and re-layouts, local(): picked = jnp.take_along_axis(flattened, own_places, axis=2)  14.3 us
    all_to_all x1, starting transfers between devices, swapped_in(): parts = lax.all_to_all(parts, name, split_axis=0, concat_axis=0)  7.31 us
    psum x1, blocking collectives, local(): total_sq = lax.psum(jnp.sum(update * update), 'mp')  6.27 us
    dot_general x2, matrix products, inverse_dct(): jnp.einsum('kr,bkf->brf', table, across, precision=lax.Precision.HIGHEST)  3.78 us
    dot_general x2, matrix products, inverse_dct(): jnp.einsum('bkgl,ls->bkgs', grouped, paired, precision=lax.Precision.HIGH...  2.92 us
    dot_general x1, matrix products, forward_dct(): jnp.einsum('kr,brf->bkf', table, field, precision=lax.Precision.HIGHEST)  2.51 us
  transfers between devices with their start and end apart: 1, of which 0 were waited for; matrix products, arithmetic and copies ran while one was open for 8% of the time, Pallas kernels for 0%

profile of v1, /device:TPU:0, one launch (start us, length us, event | category | flops | bytes accessed | tf_op | source)
XLA Modules:
  0.0 110.6 jit_solution(11382678414426825892)
XLA Ops:
  0.7 0.7 fusion.34
  1.4 0.8 copy.29
  2.7 2.5 %convolution_bitcast_fusion.1 = f32[1,64,3584]{2,1,0:T(8,128)S(1)} fusion(bf16[1,64,3584]{2,1,0:T(8,128)(2,1)} %param.4, f32[1,64,3584]{2,1,0:T(8,128)} %param.5, f32[64]{0:T(128)S(1)} %get-tuple-element.9, f32[64]{0:T(128)S(1)} %get-tuple-element.8), kind=kOutput, calls=%fused_computation.6 | convolution fusion | flops 176861184 | bytes 2294272 | tf_op jit(solution)/shard_map/kr,brf->bkf/dot_general | solution.py:31
  5.4 1.5 %fusion.18 = f32[64,28,128]{2,0,1:T(8,128)S(1)} fusion(f32[128,128,1]{1,0,2:T(8,128)S(1)} %reshape.463, f32[64,28,128]{2,1,0:T(8,128)S(1)} %reshape.445), kind=kOutput, calls=%fused_computation.25 | convolution fusion | flops 352321536 | bytes 1900544 | tf_op jit(solution)/shard_map/bkgs,ls->bkgl/dot_general | solution.py:33
  6.9 0.5 copy.31
  7.5 0.3 reshape_reshape.2
  7.8 1.6 %copy.32 = f32[1,56,64,64]{3,2,1,0:T(8,128)} copy(f32[1,56,64,64]{3,1,2,0:T(8,128)S(1)} %bitcast.120) | data formatting | bytes 1835008 | tf_op jit(solution)/shard_map/transpose | solution.py:48
  9.4 2.1 %reshape.451 = f32[56,4096]{1,0:T(8,128)S(1)} reshape(f32[1,56,64,64]{3,2,1,0:T(8,128)} %copy.32) | data formatting | bytes 1835008 | tf_op jit(solution)/shard_map/reshape | solution.py:86
  11.4 14.0 %gather_fusion = f32[1792]{0:T(1024)S(1)} fusion(f32[56,4096]{1,0:T(8,128)S(1)} %reshape.451, s32[1792]{0:T(1024)S(1)} %reshape.453), kind=kCustom, calls=%fused_computation | custom fusion | bytes 28672 | tf_op jit(solution)/shard_map/jit(take_along_axis)/gather | solution.py:88
  25.6 0.8 reshape.466
  26.4 7.3 %all-to-all-start = ((f32[8,1,1792]{2,1,0:T(1,128)}), f32[8,1,1792]{2,1,0:T(1,128)}, u32[]{:S(2)}, u32[]{:S(2)}) async-start(f32[8,1,1792]{2,1,0:T(1,128)} %reshape.466), calls=%async_computation | async-start | bytes 114688 | tf_op jit(solution)/shard_map/all_to_all | solution.py:13
  33.8 31.2 %all_gather.3 = f32[8,1,56,32]{2,3,1,0:T(8,128)S(1)} all-gather(f32[1,1,56,32]{2,3,1,0:T(8,128)S(1)} %convert_element_type.28), channel_id=1, replica_groups=mesh['dp'=8,'mp'=4] {'dp'}, dimensions={0}, use_global_device_ids=true | all-gather | bytes 64512 | tf_op jit(solution)/shard_map/all_gather | solution.py:94
  65.1 3.1 %convolution_bitcast_fusion.2 = f32[1,64,56,64]{3,1,2,0:T(8,128)S(1)} fusion(s32[56,32]{1,0:T(8,128)S(1)} %get-tuple-element.5, f32[56,32]{1,0:T(8,128)S(1)} %and_select_fusion, s32[56,32]{1,0:T(8,128)S(1)} %get-tuple-element.4), kind=kOutput, calls=%fused_computation.12 | convolution fusion | flops 88424448 | bytes 939008 | tf_op jit(solution)/shard_map/nbcjk,nbcjl->bckl/dot_general | solution.py:60
  68.2 1.1 copy.34
  69.6 1.5 %convolution_bitcast_fusion.4 = f32[28,8,8,128]{3,2,1,0:T(8,128)S(1)} fusion(f32[128,128,1]{1,0,2:T(8,128)S(1)} %reshape.463, f32[64,28,128]{2,1,0:T(8,128)S(1)} %reshape.447), kind=kOutput, calls=%fused_computation.15 | convolution fusion | flops 352321536 | bytes 1900544 | tf_op jit(solution)/shard_map/bkgl,ls->bkgs/dot_general | solution.py:40
  71.1 2.0 %fusion.2 = f32[1,64,3584]{2,1,0:T(8,128)} fusion(f32[28,8,8,128]{3,2,1,0:T(8,128)S(1)} %convolution_bitcast_fusion.4, bf16[1,64,3584]{2,1,0:T(8,128)(2,1)S(1)} %copy-done.1, f32[1,64,3584]{2,1,0:T(8,128)S(1)} %copy-done, f32[64]{0:T(128)S(1)} %get-tuple-element.9, f32[64]{0:T(128)S(1)} %get-tuple-element.8), kind=kOutput, calls=%fused_computation.7 | convolution fusion | flops 177090560 | bytes 3211776 | tf_op jit(solution)/shard_map/kr,bkf->brf/dot_general | solution.py:42
  73.5 0.5 broadcast.365
  74.0 1.6 %reduce.3 = f32[8,1792]{1,0:T(8,128)S(1)} reduce(f32[8,1,1792]{2,1,0:T(1,128)} %all-to-all-done, f32[]{:T(128)} %broadcast.365), dimensions={1}, to_apply=%all_to_all.3.reduce_sub_computation | reduce | bytes 114692 | tf_op jit(solution)/shard_map/all_to_all | solution.py:13
  75.9 22.1 %fusion.7 = f32[1,64,56,64]{3,1,2,0:T(8,128)S(1)} fusion(s32[8,56,32]{2,0,1:T(8,128)S(1)} %copy.43, f32[8,56,32]{2,0,1:T(8,128)S(1)} %copy.42, s32[8,56,32]{2,0,1:T(8,128)S(1)} %copy.37), kind=kOutput, calls=%fused_computation.13 | convolution fusion | flops 707395584 | bytes 1089536 | tf_op jit(solution)/shard_map/nbcjk,nbcjl->bckl/dot_general | solution.py:60
  98.0 1.1 copy.44
  99.4 1.5 %convolution_bitcast_fusion.3 = f32[28,8,8,128]{3,2,1,0:T(8,128)S(1)} fusion(f32[128,128,1]{1,0,2:T(8,128)S(1)} %reshape.463, f32[64,28,128]{2,1,0:T(8,128)S(1)} %reshape.449), kind=kOutput, calls=%fused_computation.14 | convolution fusion | flops 352321536 | bytes 1900544 | tf_op jit(solution)/shard_map/bkgl,ls->bkgs/dot_general | solution.py:40
  100.9 1.8 %multiply_reduce_fusion = (f32[]{:T(128)}, f32[3584,64]{0,1:T(8,128)S(1)}) fusion(f32[64]{0:T(128)S(1)} %get-tuple-element.9, f32[64]{0:T(128)S(1)} %get-tuple-element.8, f32[28,8,8,128]{3,2,1,0:T(8,128)S(1)} %convolution_bitcast_fusion.3), kind=kOutput, calls=%fused_computation.27 | convolution fusion | flops 176631808 | bytes 1835524 | tf_op jit(solution)/shard_map/kr,bkf->brf/dot_general | solution.py:42
  102.6 6.3 %psum.7 = f32[]{:T(128)} all-reduce(f32[]{:T(128)} %get-tuple-element.6), channel_id=1, replica_groups=mesh['dp'=8,'mp'=4] {'mp'}, use_global_device_ids=true, to_apply=%region_1.2 | all-reduce | flops 1 | bytes 8 | tf_op jit(solution)/shard_map/psum | solution.py:99
  109.6 1.0 bitcast_subtract_fusion
  (33 shorter events, 2.3 us)
Async XLA Ops:
  11.4 22.3 %copy-start.3 = (s32[1,1,56,32]{2,3,1,0:T(8,128)S(1)}, s32[1,1,56,32]{2,3,1,0:T(8,128)}, u32[]{:S(2)}) copy-start(s32[1,1,56,32]{2,3,1,0:T(8,128)} %param.7) | copy-start | bytes 21508
  26.4 47.1 %all-to-all-start = ((f32[8,1,1792]{2,1,0:T(1,128)}), f32[8,1,1792]{2,1,0:T(1,128)}, u32[]{:S(2)}, u32[]{:S(2)}) async-start(f32[8,1,1792]{2,1,0:T(1,128)} %reshape.466), calls=%async_computation | async-start | bytes 114688 | tf_op jit(solution)/shard_map/all_to_all | solution.py:13
  69.2 1.8 %copy-start.1 = (bf16[1,64,3584]{2,1,0:T(8,128)(2,1)S(1)}, bf16[1,64,3584]{2,1,0:T(8,128)(2,1)}, u32[]{:S(2)}) copy-start(bf16[1,64,3584]{2,1,0:T(8,128)(2,1)} %param.4) | copy-start | bytes 1376260
  69.6 1.5 %copy-start = (f32[1,64,3584]{2,1,0:T(8,128)S(1)}, f32[1,64,3584]{2,1,0:T(8,128)}, u32[]{:S(2)}) copy-start(f32[1,64,3584]{2,1,0:T(8,128)} %param.5) | copy-start | bytes 2752516
  100.9 8.7 %copy-start.2 = (f32[64,3584]{1,0:T(8,128)S(1)}, f32[64,3584]{1,0:T(8,128)}, u32[]{:S(2)}) copy-start(f32[64,3584]{1,0:T(8,128)} %param.6) | copy-start | bytes 2752516
